TPU v7x, 32 devices: a whole 2x2x4 slice. The times are simulated.
32 devices in a mesh: batch: 8 (over z, x), seq: 4 (over y, core).
Axes of the slice: x: 2, y: 2, z: 4, core: 2. Of those that a mesh axis runs over, the one named last changes fastest.
Arguments:
- hidden_in: bfloat16 [8, 512, 2048], P('batch', 'seq'), may hold values from -6 to 6
- queries: bfloat16 [8, 512, 2048], P('batch', 'seq'), may hold values from -5 to 5
- key_states: bfloat16 [8, 512, 512], P('batch', 'seq'), may hold values from -12 to 12
- value_states: bfloat16 [8, 512, 512], P('batch', 'seq'), may hold values from -6 to 6
- grad_out: bfloat16 [8, 512, 2048], P('batch', 'seq'), may hold values from -6 to 6
- log_sums: float32 [8, 16, 512], P('batch', None, 'seq'), may hold values from -700 to 700, as said below
- deltas: float32 [8, 16, 512], P('batch', None, 'seq'), may hold values from -6 to 6
- block_order: int32 [8], replicated, may hold values from 0 to 7, as said below
Outputs:
- grad_queries: bfloat16 [8, 512, 2048], P('batch', 'seq')
- grad_keys: bfloat16 [8, 512, 512], P('batch', 'seq')
- grad_values: bfloat16 [8, 512, 512], P('batch', 'seq')
- key_wgrad: float32 [2048, 512], P(('batch', 'seq'))
- value_wgrad: float32 [2048, 512], P(('batch', 'seq'))
Inputs may be any that keep to these rules, and one draw needn't show every extreme that they name: `block_order`: entries 2i and 2i+1 name blocks c and 7 - c for some c, in either order; the 8 entries together are a permutation of 0 to 7. `log_sums`: each entry lies within 0.1 of the log of the sum over visible j of exp(scores[b,h,i,j]).
All inputs are finite; a program needn't handle non-finite values.
Results may differ from a plain program's by a relative error of at most 0.0049.
Values may be sent and summed in bfloat16 or wider, within the bound.
No kernel may reach another device: no remote copies, remote signals or barrier semaphores. Data moves between devices by JAX's collectives and lax.ppermute only.
A program may use at most 64 MiB of HBM per device.

v0:
```python
import math

import jax
import jax.numpy as jnp
from jax import lax
from jax.experimental import pallas as pl
from jax.experimental.pallas import tpu as pltpu
from jax.sharding import PartitionSpec as P

HQ = 16
HK = 4
DH = 128


MASKED = -1e30


def passed_along(value, axis, steps):
    count = lax.axis_size(axis)
    pairs = [(source, (source + steps) % count) for source in range(count)]
    return lax.ppermute(value, axis, pairs)


def stored_positions(block_order, first_row, row_count, span_rows):
    row_ids = first_row + jnp.arange(row_count, dtype=jnp.int32)
    slot_ids = row_ids // span_rows
    matches = slot_ids[:, None] == jnp.arange(block_order.shape[0], dtype=jnp.int32)[None, :]
    block_ids = jnp.sum(jnp.where(matches, block_order[None, :], 0), axis=1)
    return block_ids * span_rows + row_ids % span_rows


def head_scores(left_heads, right_block):
    batch_rows, right_rows = (right_block.shape[0], right_block.shape[1])
    right_heads = right_block.reshape(batch_rows, right_rows, HK, DH)
    return jnp.einsum(
        "bqhgd,bkhd->bhgqk", left_heads, right_heads, preferred_element_type=jnp.float32
    )


def masked_scores(query_heads, key_block, query_pos, key_pos):
    scores = head_scores(query_heads, key_block) * (1.0 / math.sqrt(DH))
    visible = key_pos[None, :] <= query_pos[:, None]
    return jnp.where(visible, scores, MASKED)


def grad_block(
    query_heads, grad_heads, query_pos, row_lse, row_deltas, key_block, value_block, key_pos
):
    scores = masked_scores(query_heads, key_block, query_pos, key_pos)
    probs = jnp.exp(scores - row_lse[..., None])
    grad_probs = head_scores(grad_heads, value_block)
    grad_scores = (probs * (grad_probs - row_deltas[..., None]) * (1.0 / math.sqrt(DH))).astype(
        jnp.bfloat16
    )
    probs_low = probs.astype(jnp.bfloat16)
    batch_rows, key_rows = (key_block.shape[0], key_block.shape[1])
    key_heads = key_block.reshape(batch_rows, key_rows, HK, DH)
    query_part = jnp.einsum(
        "bhgqk,bkhd->bqhgd", grad_scores, key_heads, preferred_element_type=jnp.float32
    )
    key_part = jnp.einsum(
        "bhgqk,bqhgd->bkhd", grad_scores, query_heads, preferred_element_type=jnp.float32
    )
    value_part = jnp.einsum(
        "bhgqk,bqhgd->bkhd", probs_low, grad_heads, preferred_element_type=jnp.float32
    )
    key_part = key_part.reshape(batch_rows, key_rows, HK * DH)
    value_part = value_part.reshape(batch_rows, key_rows, HK * DH)
    return (query_part, key_part, value_part)


def ring_shards(hidden_in, queries, key_states, value_states, grad_out, log_sums, deltas, block_order):
    seq_count = lax.axis_size("seq")
    my_index = lax.axis_index("seq")
    batch_rows, local_rows = (queries.shape[0], queries.shape[1])
    span_rows = local_rows // 2
    group_size = HQ // HK
    query_heads = queries.reshape(batch_rows, local_rows, HK, group_size, DH)
    grad_heads = grad_out.reshape(batch_rows, local_rows, HK, group_size, DH)
    row_lse = log_sums.reshape(batch_rows, HK, group_size, local_rows)
    row_deltas = deltas.reshape(batch_rows, HK, group_size, local_rows)
    query_pos = stored_positions(block_order, my_index * local_rows, local_rows, span_rows)
    key_zeros = jnp.zeros(key_states.shape, jnp.float32)
    query_zeros = jnp.zeros(query_heads.shape, jnp.float32)

    def block_grads(accums, key_block, value_block, source):
        key_acc, value_acc, query_acc = accums
        key_pos = stored_positions(block_order, source * local_rows, local_rows, span_rows)
        query_part, key_part, value_part = grad_block(
            query_heads, grad_heads, query_pos, row_lse, row_deltas, key_block, value_block, key_pos
        )
        return (key_acc + key_part, value_acc + value_part, query_acc + query_part)

    whole_keys, whole_values = (
        lax.all_gather(key_states, "seq", axis=1, tiled=True),
        lax.all_gather(value_states, "seq", axis=1, tiled=True),
    )

    def back_turn(turn_index, accums):
        source = (my_index + turn_index + 1) % seq_count
        key_block = lax.dynamic_slice_in_dim(whole_keys, source * local_rows, local_rows, 1)
        value_block = lax.dynamic_slice_in_dim(whole_values, source * local_rows, local_rows, 1)
        return block_grads(accums, key_block, value_block, source)

    def back_step(turn_index, accums):
        key_acc, value_acc, query_acc = back_turn(turn_index, accums)
        key_acc, value_acc = passed_along((key_acc, value_acc), "seq", -1)
        return (key_acc, value_acc, query_acc)

    accums = lax.fori_loop(0, seq_count - 1, back_step, (key_zeros, key_zeros, query_zeros))
    key_acc, value_acc, query_acc = back_turn(seq_count - 1, accums)
    grad_keys = key_acc.astype(jnp.bfloat16)
    grad_values = value_acc.astype(jnp.bfloat16)
    grad_queries = query_acc.reshape(batch_rows, local_rows, HQ * DH).astype(jnp.bfloat16)
    key_width = HK * DH
    token_grads = jnp.concatenate([grad_keys, grad_values], axis=2).reshape(
        batch_rows * local_rows, 2 * key_width
    )
    flat_hidden = hidden_in.reshape(batch_rows * local_rows, hidden_in.shape[2])
    weight_grads = lax.psum_scatter(
        jnp.einsum("td,te->de", flat_hidden, token_grads, preferred_element_type=jnp.float32),
        ("batch", "seq"),
        scatter_dimension=0,
        tiled=True,
    )
    return (
        grad_queries,
        grad_keys,
        grad_values,
        weight_grads[:, :key_width],
        weight_grads[:, key_width:],
    )


def swapped(value, axis, distance):
    count = lax.axis_size(axis)
    return lax.ppermute(value, axis, [(source, source ^ distance) for source in range(count)])


def dot(left, right, left_dim, right_dim):
    dims = (((left_dim,), (right_dim,)), ((), ()))
    return lax.dot_general(left, right, dims, preferred_element_type=jnp.float32)


def vmem():
    return pl.BlockSpec(memory_space=pltpu.VMEM)


def smem():
    return pl.BlockSpec(memory_space=pltpu.SMEM)


def call(body, out_shapes, operands, scalars, scratch=(), after=()):
    specs = [smem()] * scalars + [vmem()] * (len(operands) - scalars)
    specs += [pl.BlockSpec(memory_space=pl.ANY)] * len(after)
    outs = pl.pallas_call(
        body,
        out_shape=out_shapes,
        in_specs=specs,
        out_specs=[vmem()] * len(out_shapes),
        scratch_shapes=scratch,
    )(*operands, *after)
    return list(outs)


def shaped(shape, dtype=jnp.bfloat16):
    return jax.ShapeDtypeStruct(shape, dtype)


def head_payloads(place, queries, grad_out, keys, values, log_sums, deltas, count):
    rows, query_width = queries.shape
    key_width = keys.shape[1]
    query_part, key_part = (query_width // count, key_width // count)
    heads = log_sums.shape[0]
    part = heads // count

    def pack_heads(place_ref, query_ref, grad_ref, key_ref, value_ref, lse_ref, delta_ref, *refs):
        out_refs, term_refs = (refs[:count], refs[count:])

        def own_heads(source_ref, peer):
            chosen = source_ref[:part, :]
            for index in range(1, count):
                chosen = jnp.where(
                    peer == index, source_ref[index * part : (index + 1) * part, :], chosen
                )
            return chosen

        for distance, out_ref in enumerate(out_refs):
            peer = place_ref[0] ^ distance
            wide = pl.ds(pl.multiple_of(peer * query_part, query_part), query_part)
            thin = pl.ds(pl.multiple_of(peer * key_part, key_part), key_part)
            out_ref[:, :query_part] = query_ref[:, wide]
            out_ref[:, query_part : 2 * query_part] = grad_ref[:, wide]
            out_ref[:, 2 * query_part : 2 * query_part + key_part] = key_ref[:, thin]
            out_ref[:, 2 * query_part + key_part :] = value_ref[:, thin]
            term_refs[distance][:part, :] = own_heads(lse_ref, peer)
            term_refs[distance][part:, :] = own_heads(delta_ref, peer)

    shapes = [shaped((rows, 2 * query_part + 2 * key_part))] * count
    shapes += [shaped((2 * part, rows), jnp.float32)] * count
    operands = (place, queries, grad_out, keys, values, log_sums, deltas)
    outs = call(pack_heads, shapes, operands, 1)
    return (outs[:count], outs[count:])


def feature_payloads(place, hidden, count, owners, after):
    rows, width = hidden.shape
    own = width // (count * owners)

    def pack_features(place_ref, hidden_ref, _, *refs):
        out_refs, turned_ref = (refs[:-1], refs[-1])
        turned_ref[...] = hidden_ref[...].T
        for distance, out_ref in enumerate(out_refs):
            peer = place_ref[0] ^ distance
            for owner in range(owners):
                first = pl.multiple_of((owner * count + peer) * own, own)
                out_ref[owner * own : (owner + 1) * own, :] = turned_ref[pl.ds(first, own), :]

    shape = shaped((owners * own, rows))
    scratch = [pltpu.VMEM((width, rows), jnp.bfloat16)]
    return call(pack_features, [shape] * count, (place, hidden), 1, scratch, (after,))


def head_grads(place, order, payloads, row_terms, span_rows, after):
    count = len(payloads)
    rows = payloads[0].shape[0]
    group_size = row_terms[0].shape[0] // 2
    total = count * rows
    spans = total // span_rows
    held = rows // span_rows
    tile = min(total, 256)
    query_part = group_size * DH

    def attention_grads(place_ref, order_ref, *refs):
        data_refs, term_refs = (refs[:count], refs[count : 2 * count])
        query_refs, token_ref = (refs[2 * count + 1 : 3 * count + 1], refs[3 * count + 1])

        def positions(shape, dim):
            ids = lax.broadcasted_iota(jnp.int32, shape, dim)
            result = ids % span_rows
            slots = ids // span_rows
            for span in range(spans):
                stored = (place_ref[0] ^ (span // held)) * held + span % held
                result = jnp.where(slots == span, result + order_ref[stored] * span_rows, result)
            return result

        def columns(first):
            return jnp.concatenate([ref[:, first : first + DH] for ref in data_refs], axis=0)

        query_pos = positions((1, total), 1)
        key_pos = positions((total, 1), 0)
        keys = columns(2 * query_part)
        values = columns(2 * query_part + DH)
        scale = 1.0 / math.sqrt(DH)
        hidden_add = [
            jnp.where(key_pos[first : first + tile] <= query_pos, 0.0, MASKED)
            for first in range(0, total, tile)
        ]
        key_sums = [None] * (total // tile)
        value_sums = [None] * (total // tile)
        for head in range(group_size):
            queries = columns(head * DH)
            grads = columns(query_part + head * DH)
            lse = jnp.concatenate([ref[head : head + 1, :] for ref in term_refs], axis=1)
            deltas = jnp.concatenate(
                [ref[group_size + head : group_size + head + 1, :] for ref in term_refs], axis=1
            )
            query_sum = None
            for index in range(total // tile):
                part = slice(index * tile, (index + 1) * tile)
                scores = dot(keys[part], queries, 1, 1) * scale + hidden_add[index]
                probs = jnp.exp(scores - lse)
                grad_probs = dot(values[part], grads, 1, 1)
                grad_scores = (probs * (grad_probs - deltas) * scale).astype(jnp.bfloat16)
                key_part = dot(grad_scores, queries, 1, 0)
                value_part = dot(probs.astype(jnp.bfloat16), grads, 1, 0)
                query_tile = dot(grad_scores, keys[part], 0, 0)
                query_sum = query_tile if index == 0 else query_sum + query_tile
                key_sums[index] = key_part if head == 0 else key_sums[index] + key_part
                value_sums[index] = value_part if head == 0 else value_sums[index] + value_part
            for source, out_ref in enumerate(query_refs):
                out_ref[:, head * DH : (head + 1) * DH] = query_sum[
                    source * rows : (source + 1) * rows
                ].astype(jnp.bfloat16)
        for index in range(total // tile):
            part = slice(index * tile, (index + 1) * tile)
            token_ref[part, :DH] = key_sums[index].astype(jnp.bfloat16)
            token_ref[part, DH:] = value_sums[index].astype(jnp.bfloat16)

    shapes = [shaped((rows, query_part))] * count + [shaped((total, 2 * DH))]
    outs = call(attention_grads, shapes, (place, order, *payloads, *row_terms), 2, (), (after,))
    return (outs[:count], outs[count])


def weight_parts(owner, features, tokens, owners):
    count = len(features)
    width, rows = features[0].shape
    own = width // owners
    shifts = [shift for shift, _ in tokens]

    def weight_grads(owner_ref, *refs):
        feature_refs, token_refs = (refs[:count], refs[count : count + len(shifts)])
        own_ref, part_refs, sum_ref = (refs[count + len(shifts)], refs[count + len(shifts) + 1 : -1], refs[-1])
        left = jnp.concatenate([ref[...] for ref in feature_refs], axis=1)
        for column, (shift, token_ref) in enumerate(zip(shifts, token_refs)):
            right = jnp.concatenate(
                [
                    token_ref[(shift ^ source) * rows : ((shift ^ source) + 1) * rows, :]
                    for source in range(count)
                ],
                axis=0,
            )
            sum_ref[:, column * 2 * DH : (column + 1) * 2 * DH] = dot(left, right, 1, 0)
        first = pl.multiple_of(owner_ref[0] * own, own)
        own_ref[...] = sum_ref[pl.ds(first, own), :]
        for index, part_ref in enumerate(part_refs):
            first = pl.multiple_of((owner_ref[0] ^ (index + 1)) * own, own)
            part_ref[...] = sum_ref[pl.ds(first, own), :].astype(jnp.bfloat16)

    columns = len(shifts) * 2 * DH
    shapes = [shaped((own, columns), jnp.float32)] + [shaped((own, columns))] * (owners - 1)
    scratch = [pltpu.VMEM((width, columns), jnp.float32)]
    operands = (owner, *features, *[held for _, held in tokens])
    outs = call(weight_grads, shapes, operands, 1, scratch)
    return (outs[0], outs[1:])


def summed(own, parts):
    def sum_parts(own_ref, *refs):
        total = own_ref[...]
        for part_ref in refs[:-1]:
            total = total + part_ref[...].astype(jnp.float32)
        refs[-1][...] = total

    return call(sum_parts, [shaped(own.shape, jnp.float32)], (own, *parts), 0)[0]


def summed_last(place, done, own, parts, count):
    rows, width = own.shape

    def sum_last_parts(place_ref, *refs):
        done_refs, own_ref = (refs[: len(done)], refs[len(done)])
        part_refs, key_ref, value_ref = (refs[len(done) + 1 : -2], refs[-2], refs[-1])
        last = own_ref[...]
        for part_ref in part_refs:
            last = last + part_ref[...].astype(jnp.float32)
        pieces = [ref[...] for ref in done_refs] + [last]
        for index, piece in enumerate(pieces):
            for column in range(width // (2 * DH)):
                shift = index * (width // (2 * DH)) + column
                head = pl.multiple_of((place_ref[0] ^ shift) * DH, DH)
                first = column * 2 * DH
                key_ref[:, pl.ds(head, DH)] = piece[:, first : first + DH]
                value_ref[:, pl.ds(head, DH)] = piece[:, first + DH : first + 2 * DH]

    shape = shaped((rows, count * DH), jnp.float32)
    return call(sum_last_parts, [shape] * 2, (place, *done, own, *parts), 1)


def joined_rows(place, query_parts, tokens):
    count = len(query_parts)
    rows, width = query_parts[0].shape

    def join_rows(place_ref, *refs):
        part_refs, token_refs = (refs[:count], refs[count : 2 * count])
        query_ref, key_ref, value_ref = refs[2 * count :]
        for distance in range(count):
            peer = place_ref[0] ^ distance
            wide = pl.ds(pl.multiple_of(peer * width, width), width)
            thin = pl.ds(pl.multiple_of(peer * DH, DH), DH)
            mine = slice(distance * rows, (distance + 1) * rows)
            query_ref[:, wide] = part_refs[distance][...]
            key_ref[:, thin] = token_refs[distance][mine, :DH]
            value_ref[:, thin] = token_refs[distance][mine, DH:]

    shapes = [shaped((rows, count * width))] + [shaped((rows, count * DH))] * 2
    return call(join_rows, shapes, (place, *query_parts, *tokens), 1)


def head_shards(hidden_in, queries, key_states, value_states, grad_out, log_sums, deltas, block_order):
    count = lax.axis_size("seq")
    owners = lax.axis_size("batch")
    place = lax.axis_index("seq").astype(jnp.int32).reshape(1)
    owner = lax.axis_index("batch").astype(jnp.int32).reshape(1)
    span_rows = queries.shape[1] * count // block_order.shape[0]
    far_first = sorted(range(1, count), reverse=True)

    payloads, row_terms = head_payloads(
        place, queries[0], grad_out[0], key_states[0], value_states[0], log_sums[0], deltas[0], count
    )
    features = feature_payloads(place, hidden_in[0], count, owners, payloads[0])
    local_features = features[0]
    for distance in far_first:
        row_terms[distance] = swapped(row_terms[distance], "seq", distance)
        payloads[distance] = swapped(payloads[distance], "seq", distance)
    for distance in far_first:
        features[distance] = swapped(features[distance], "seq", distance)
    query_parts, tokens = head_grads(
        place, block_order, payloads, row_terms, span_rows, local_features
    )
    held = {0: tokens}
    half = count // 2
    held[half] = swapped(tokens, "seq", half)
    step = half // 2
    while step:
        for distance in sorted(held):
            held[distance ^ step] = swapped(held[distance], "seq", step)
        step //= 2
    done = []
    for group in range(2):
        some = [(shift, held[shift]) for shift in range(group * half, (group + 1) * half)]
        own, parts = weight_parts(owner, features, some, owners)
        parts = [
            swapped(part, "batch", index + 1)
            for index, part in reversed(list(enumerate(parts)))
        ]
        if group == 0:
            done.append(summed(own, parts))
    for distance in far_first:
        query_parts[distance] = swapped(query_parts[distance], "seq", distance)
    all_tokens = [held[distance] for distance in range(count)]
    grad_queries, grad_keys, grad_values = joined_rows(place, query_parts, all_tokens)
    key_wgrad, value_wgrad = summed_last(place, done, own, parts, count)
    return (grad_queries[None], grad_keys[None], grad_values[None], key_wgrad, value_wgrad)


def shards(*args):
    count, owners = (lax.axis_size("seq"), lax.axis_size("batch"))
    own = args[0].shape[2] // (count * owners)
    fits = count == HK and owners & (owners - 1) == 0 and args[1].shape[0] == 1
    if fits and args[1].shape[1] % 128 == 0 and own % 16 == 0:
        return head_shards(*args)
    return ring_shards(*args)


def solution(mesh):
    in_specs = (
        P("batch", "seq", None),
        P("batch", "seq", None),
        P("batch", "seq", None),
        P("batch", "seq", None),
        P("batch", "seq", None),
        P("batch", None, "seq"),
        P("batch", None, "seq"),
        P(),
    )
    out_specs = (
        P("batch", "seq", None),
        P("batch", "seq", None),
        P("batch", "seq", None),
        P(("batch", "seq"), None),
        P(("batch", "seq"), None),
    )
    return jax.shard_map(shards, mesh=mesh, in_specs=in_specs, out_specs=out_specs, check_vma=False)
```

profile of v0, /device:TPU:0, one launch (start us, length us, event | category | flops | bytes accessed | tf_op | source)
XLA Modules:
  0.0 82.2 jit_solution(9617474102944349450)
XLA Ops:
  0.6 2.4 %shard_map.119 = (bf16[128,1280]{1,0:T(8,128)(2,1)}, bf16[128,1280]{1,0:T(8,128)(2,1)}, bf16[128,1280]{1,0:T(8,128)(2,1)}, bf16[128,1280]{1,0:T(8,128)(2,1)}, f3...) custom-call(s32[1]{0:T(128)} %bitcast.place_ref, bf16[128,2048]{1,0:T(8,128)(2,1)} %bitcast.12, ...), custom_call_target="tpu_custom_call" | custom-call | tf_op jit(solution)/shard_map/pallas_call | solution.py:156
  3.7 2.6 %collective-permute-start.1 = (bf16[128,1280]{1,0:T(8,128)(2,1)}, bf16[128,1280]{1,0:T(8,128)(2,1)S(1)}, u32[]{:S(2)}, u32[]{:S(2)}) collective-permute-start(bf16[128,1280]{1,0:T(8,128)(2,1)} %get-tuple-element.45), channel_id=1, source_target_pairs={{0,2},{1,3},{2,0},{3,1},{4,6},{5,7},{6,4},{7,5},{8,10},{9,11},{10,... | collective-permute-start | bytes 983048 | tf_op jit(solution)/shard_map/ppermute | solution.py:137
  6.4 1.9 %collective-permute-start.4 = (f32[8,128]{1,0:T(8,128)S(1)}, f32[8,128]{1,0:T(8,128)S(1)}, u32[]{:S(2)}, u32[]{:S(2)}) collective-permute-start(f32[8,128]{1,0:T(8,128)S(1)} %copy-done.36), channel_id=1, source_target_pairs={{0,2},{1,3},{2,0},{3,1},{4,6},{5,7},{6,4},{7,5},{8,10},{9,11},{10,... | collective-permute-start | bytes 12296 | tf_op jit(solution)/shard_map/ppermute | solution.py:137
  9.4 2.0 %shard_map.120 = (bf16[512,128]{1,0:T(8,128)(2,1)}, bf16[512,128]{1,0:T(8,128)(2,1)}, bf16[512,128]{1,0:T(8,128)(2,1)}, bf16[512,128]{1,0:T(8,128)(2,1)}) custom-call(s32[1]{0:T(128)} %bitcast.place_ref, bf16[128,2048]{1,0:T(8,128)(2,1)} %bitcast.14, bf16[128,1280]{1,0:T(8,128)(2,1)} %get-tuple-element.43._.refs_0_), custom_call_target="tpu_custom_call" | custom-call | tf_op jit(solution)/shard_map/pallas_call | solution.py:156
  11.4 10.5 %collective-permute-done.4.refs_6_ = f32[8,128]{1,0:T(8,128)S(1)} collective-permute-done((f32[8,128]{1,0:T(8,128)S(1)}, f32[8,128]{1,0:T(8,128)S(1)}, u32[]{:S(2)}, u32[]{:S(2)}) %collective-permute-start.4) | collective-permute-done | bytes 4128 | tf_op jit(solution)/shard_map/ppermute | solution.py:137
  22.9 5.8 %shard_map.121 = (bf16[128,512]{1,0:T(8,128)(2,1)}, bf16[128,512]{1,0:T(8,128)(2,1)}, bf16[128,512]{1,0:T(8,128)(2,1)}, bf16[128,512]{1,0:T(8,128)(2,1)}, bf16[512,256]{1,0:T(8,128)(2,1)}) custom-call(s32[1]{0:T(128)} %bitcast.place_ref, s32[8]{0:T(128)} %order_ref.1, bf16[128,1280]{1,0:T(8,128)(2,1)} %get-tuple-element.43._.refs_0_, ...), custom_call_target="tpu_custom_call" | custom-call | tf_op jit(solution)/shard_map/pallas_call | solution.py:156
  28.8 1.7 %collective-permute-start.10 = (bf16[512,256]{1,0:T(8,128)(2,1)}, bf16[512,256]{1,0:T(8,128)(2,1)S(1)}, u32[]{:S(2)}, u32[]{:S(2)}) collective-permute-start(bf16[512,256]{1,0:T(8,128)(2,1)} %get-tuple-element.56.refs_4_), channel_id=1, source_target_pairs={{0,2},{1,3},{2,0},{3,1},{4,6},{5,7},{6,4},{7,5},{8,10},{9,11},{10,... | collective-permute-start | bytes 786440 | tf_op jit(solution)/shard_map/ppermute | solution.py:137
  31.3 6.8 %collective-permute-done.10.refs_6_.refs_4_ = bf16[512,256]{1,0:T(8,128)(2,1)S(1)} collective-permute-done((bf16[512,256]{1,0:T(8,128)(2,1)}, bf16[512,256]{1,0:T(8,128)(2,1)S(1)}, u32[]{:S(2)}, u32[]{:S(2)}) %collective-permute-start.10) | collective-permute-done | bytes 262176 | tf_op jit(solution)/shard_map/ppermute | solution.py:137
  38.2 1.9 %collective-permute-start.14 = (bf16[512,128]{1,0:T(8,128)(2,1)S(1)}, bf16[512,128]{1,0:T(8,128)(2,1)S(1)}, u32[]{:S(2)}, u32[]{:S(2)}) collective-permute-start(bf16[512,128]{1,0:T(8,128)(2,1)S(1)} %copy-done.29), channel_id=1, source_target_pairs={{0,3},{1,2},{2,1},{3,0},{4,7},{5,6},{6,5},{7,4},{8,11},{9,10},{10,... | collective-permute-start | bytes 393224 | tf_op jit(solution)/shard_map/ppermute | solution.py:137
  40.1 1.7 %collective-permute-start.7 = (bf16[128,512]{1,0:T(8,128)(2,1)}, bf16[128,512]{1,0:T(8,128)(2,1)S(1)}, u32[]{:S(2)}, u32[]{:S(2)}) collective-permute-start(bf16[128,512]{1,0:T(8,128)(2,1)} %get-tuple-element.54), channel_id=1, source_target_pairs={{0,2},{1,3},{2,0},{3,1},{4,6},{5,7},{6,4},{7,5},{8,10},{9,11},{10,... | collective-permute-start | bytes 393224 | tf_op jit(solution)/shard_map/ppermute | solution.py:137
  41.8 2.1 %collective-permute-done.14.refs_3_ = bf16[512,128]{1,0:T(8,128)(2,1)S(1)} collective-permute-done((bf16[512,128]{1,0:T(8,128)(2,1)S(1)}, bf16[512,128]{1,0:T(8,128)(2,1)S(1)}, u32[]{:S(2)}, u32[]{:S(2)}) %collective-permute-start.14) | collective-permute-done | bytes 131104 | tf_op jit(solution)/shard_map/ppermute | solution.py:137
  43.9 1.9 %collective-permute-start.8 = (bf16[128,512]{1,0:T(8,128)(2,1)}, bf16[128,512]{1,0:T(8,128)(2,1)S(1)}, u32[]{:S(2)}, u32[]{:S(2)}) collective-permute-start(bf16[128,512]{1,0:T(8,128)(2,1)} %get-tuple-element.55), channel_id=1, source_target_pairs={{0,3},{1,2},{2,1},{3,0},{4,7},{5,6},{6,5},{7,4},{8,11},{9,10},{10,... | collective-permute-start | bytes 393224 | tf_op jit(solution)/shard_map/ppermute | solution.py:137
  46.5 2.6 %shard_map.123 = (f32[64,512]{1,0:T(8,128)}, bf16[64,512]{1,0:T(8,128)(2,1)}, bf16[64,512]{1,0:T(8,128)(2,1)}, bf16[64,512]{1,0:T(8,128)(2,1)}, bf16[64,512]{1,0...) custom-call(s32[1]{0:T(128)} %bitcast.11.owner_ref, ...), custom_call_target="tpu_custom_call" | custom-call | tf_op jit(solution)/shard_map/pallas_call | solution.py:156
  49.1 4.6 %collective-permute-start.15 = (bf16[64,512]{1,0:T(8,128)(2,1)}, bf16[64,512]{1,0:T(8,128)(2,1)S(1)}, u32[]{:S(2)}, u32[]{:S(2)}) collective-permute-start(bf16[64,512]{1,0:T(8,128)(2,1)} %get-tuple-element.64), channel_id=1, source_target_pairs={{0,28},{4,24},{8,20},{12,16},{16,12},{20,8},{24,4},{28,0},{1,29},{... | collective-permute-start | bytes 196616 | tf_op jit(solution)/shard_map/ppermute | solution.py:137
  54.7 2.2 %collective-permute-start.18 = (bf16[64,512]{1,0:T(8,128)(2,1)}, bf16[64,512]{1,0:T(8,128)(2,1)S(1)}, u32[]{:S(2)}, u32[]{:S(2)}) collective-permute-start(bf16[64,512]{1,0:T(8,128)(2,1)} %get-tuple-element.67), channel_id=1, source_target_pairs={{0,16},{4,20},{8,24},{12,28},{16,0},{20,4},{24,8},{28,12},{1,17},{... | collective-permute-start | bytes 196616 | tf_op jit(solution)/shard_map/ppermute | solution.py:137
  56.9 2.6 %shard_map.125 = (f32[64,512]{1,0:T(8,128)}, bf16[64,512]{1,0:T(8,128)(2,1)}, bf16[64,512]{1,0:T(8,128)(2,1)}, bf16[64,512]{1,0:T(8,128)(2,1)}, bf16[64,512]{1,0...) custom-call(s32[1]{0:T(128)} %bitcast.11.owner_ref, ...), custom_call_target="tpu_custom_call" | custom-call | tf_op jit(solution)/shard_map/pallas_call | solution.py:156
  59.5 2.8 %collective-permute-start.19 = (bf16[64,512]{1,0:T(8,128)(2,1)S(1)}, bf16[64,512]{1,0:T(8,128)(2,1)S(1)}, u32[]{:S(2)}, u32[]{:S(2)}) collective-permute-start(bf16[64,512]{1,0:T(8,128)(2,1)S(1)} %copy-done.34), channel_id=1, source_target_pairs={{0,12},{4,8},{8,4},{12,0},{16,28},{20,24},{24,20},{28,16},{1,13},{... | collective-permute-start | bytes 196616 | tf_op jit(solution)/shard_map/ppermute | solution.py:137
  63.2 4.5 %collective-permute-start.22 = (bf16[64,512]{1,0:T(8,128)(2,1)}, bf16[64,512]{1,0:T(8,128)(2,1)S(1)}, u32[]{:S(2)}, u32[]{:S(2)}) collective-permute-start(bf16[64,512]{1,0:T(8,128)(2,1)} %get-tuple-element.72), channel_id=1, source_target_pairs={{0,28},{4,24},{8,20},{12,16},{16,12},{20,8},{24,4},{28,0},{1,29},{... | collective-permute-start | bytes 196616 | tf_op jit(solution)/shard_map/ppermute | solution.py:137
  68.7 2.2 %collective-permute-start.25 = (bf16[64,512]{1,0:T(8,128)(2,1)}, bf16[64,512]{1,0:T(8,128)(2,1)S(1)}, u32[]{:S(2)}, u32[]{:S(2)}) collective-permute-start(bf16[64,512]{1,0:T(8,128)(2,1)} %get-tuple-element.75), channel_id=1, source_target_pairs={{0,16},{4,20},{8,24},{12,28},{16,0},{20,4},{24,8},{28,12},{1,17},{... | collective-permute-start | bytes 196616 | tf_op jit(solution)/shard_map/ppermute | solution.py:137
  70.9 2.3 %collective-permute-start.26 = (bf16[64,512]{1,0:T(8,128)(2,1)}, bf16[64,512]{1,0:T(8,128)(2,1)S(1)}, u32[]{:S(2)}, u32[]{:S(2)}) collective-permute-start(bf16[64,512]{1,0:T(8,128)(2,1)} %get-tuple-element.76), channel_id=1, source_target_pairs={{0,12},{4,8},{8,4},{12,0},{16,28},{20,24},{24,20},{28,16},{1,13},{... | collective-permute-start | bytes 196616 | tf_op jit(solution)/shard_map/ppermute | solution.py:137
  73.2 1.4 %collective-permute-start.27 = (bf16[64,512]{1,0:T(8,128)(2,1)}, bf16[64,512]{1,0:T(8,128)(2,1)S(1)}, u32[]{:S(2)}, u32[]{:S(2)}) collective-permute-start(bf16[64,512]{1,0:T(8,128)(2,1)} %get-tuple-element.77), channel_id=1, source_target_pairs={{0,8},{4,12},{8,0},{12,4},{16,24},{20,28},{24,16},{28,20},{1,9},{5... | collective-permute-start | bytes 196616 | tf_op jit(solution)/shard_map/ppermute | solution.py:137
  75.4 1.8 %shard_map.124.refs_0_ = f32[64,512]{1,0:T(8,128)} custom-call(f32[64,512]{1,0:T(8,128)} %get-tuple-element.63.own_ref, bf16[64,512]{1,0:T(8,128)(2,1)} %copy-done.19, bf16[64,512]{1,0:T(8,128)(2,1)} %copy-done.20, bf16[64,512]{1,0:T(8,128)(2,1)} %copy-done.21, bf16[64,512]{1,0:T(8,128)(2,1)} %copy-done.22, bf16[64,512]{1,0:T(8,128)(2,1)} %copy-done.23, ...), custom_call_target="tpu_custom_call" | custom-call | tf_op jit(solution)/shard_map/pallas_call | solution.py:156
  77.3 2.3 %shard_map.122 = (bf16[128,2048]{1,0:T(8,128)(2,1)}, bf16[128,512]{1,0:T(8,128)(2,1)}, bf16[128,512]{1,0:T(8,128)(2,1)}) custom-call(s32[1]{0:T(128)} %bitcast.place_ref, bf16[128,512]{1,0:T(8,128)(2,1)} %get-tuple-element.52.refs_0_, bf16[128,512]{1,0:T(8,128)(2,1)} %copy-done.9, bf16[128,512]{1,0:T(8,128)(2,1)} %copy-done.10, bf16[128,512]{1,0:T(8,128)(2,1)} %copy-done.11, ...), custom_call_target="tpu_custom_call" | custom-call | tf_op jit(solution)/shard_map/pallas_call | solution.py:156
  80.4 1.9 %shard_map.126 = (f32[64,512]{1,0:T(8,128)}, f32[64,512]{1,0:T(8,128)}) custom-call(s32[1]{0:T(128)} %bitcast.place_ref, f32[64,512]{1,0:T(8,128)} %shard_map.124.refs_0_, f32[64,512]{1,0:T(8,128)} %get-tuple-element.71.refs_1_, bf16[64,512]{1,0:T(8,128)(2,1)} %copy-done.12, bf16[64,512]{1,0:T(8,128)(2,1)} %copy-done.13, bf16[64,512]{1,0:T(8,128)(2,1)} %copy-done.14, ...), custom_call_target="tpu_custom_call" | custom-call | tf_op jit(solution)/shard_map/pallas_call | solution.py:156
  (116 shorter events, 8.6 us)
Async XLA Ops:
  3.1 18.8 %collective-permute-start = (bf16[128,1280]{1,0:T(8,128)(2,1)}, bf16[128,1280]{1,0:T(8,128)(2,1)S(1)}, u32[]{:S(2)}, u32[]{:S(2)}) collective-permute-start(bf16[128,1280]{1,0:T(8,128)(2,1)} %get-tuple-element.44), channel_id=1, source_target_pairs={{0,1},{1,0},{2,3},{3,2},{4,5},{5,4},{6,7},{7,6},{8,9},{9,8},{10,11... | collective-permute-start | bytes 983048 | tf_op jit(solution)/shard_map/ppermute | solution.py:137
  3.7 18.3 %collective-permute-start.1 = (bf16[128,1280]{1,0:T(8,128)(2,1)}, bf16[128,1280]{1,0:T(8,128)(2,1)S(1)}, u32[]{:S(2)}, u32[]{:S(2)}) collective-permute-start(bf16[128,1280]{1,0:T(8,128)(2,1)} %get-tuple-element.45), channel_id=1, source_target_pairs={{0,2},{1,3},{2,0},{3,1},{4,6},{5,7},{6,4},{7,5},{8,10},{9,11},{10,... | collective-permute-start | bytes 983048 | tf_op jit(solution)/shard_map/ppermute | solution.py:137
  6.2 15.7 %collective-permute-start.2 = (bf16[128,1280]{1,0:T(8,128)(2,1)}, bf16[128,1280]{1,0:T(8,128)(2,1)S(1)}, u32[]{:S(2)}, u32[]{:S(2)}) collective-permute-start(bf16[128,1280]{1,0:T(8,128)(2,1)} %get-tuple-element.46), channel_id=1, source_target_pairs={{0,3},{1,2},{2,1},{3,0},{4,7},{5,6},{6,5},{7,4},{8,11},{9,10},{10,... | collective-permute-start | bytes 983048 | tf_op jit(solution)/shard_map/ppermute | solution.py:137
  6.4 15.5 %collective-permute-start.4 = (f32[8,128]{1,0:T(8,128)S(1)}, f32[8,128]{1,0:T(8,128)S(1)}, u32[]{:S(2)}, u32[]{:S(2)}) collective-permute-start(f32[8,128]{1,0:T(8,128)S(1)} %copy-done.36), channel_id=1, source_target_pairs={{0,2},{1,3},{2,0},{3,1},{4,6},{5,7},{6,4},{7,5},{8,10},{9,11},{10,... | collective-permute-start | bytes 12296 | tf_op jit(solution)/shard_map/ppermute | solution.py:137
  8.4 13.5 %collective-permute-start.5 = (f32[8,128]{1,0:T(8,128)S(1)}, f32[8,128]{1,0:T(8,128)S(1)}, u32[]{:S(2)}, u32[]{:S(2)}) collective-permute-start(f32[8,128]{1,0:T(8,128)S(1)} %copy-done.35), channel_id=1, source_target_pairs={{0,3},{1,2},{2,1},{3,0},{4,7},{5,6},{6,5},{7,4},{8,11},{9,10},{10,... | collective-permute-start | bytes 12296 | tf_op jit(solution)/shard_map/ppermute | solution.py:137
  28.8 9.4 %collective-permute-start.10 = (bf16[512,256]{1,0:T(8,128)(2,1)}, bf16[512,256]{1,0:T(8,128)(2,1)S(1)}, u32[]{:S(2)}, u32[]{:S(2)}) collective-permute-start(bf16[512,256]{1,0:T(8,128)(2,1)} %get-tuple-element.56.refs_4_), channel_id=1, source_target_pairs={{0,2},{1,3},{2,0},{3,1},{4,6},{5,7},{6,4},{7,5},{8,10},{9,11},{10,... | collective-permute-start | bytes 786440 | tf_op jit(solution)/shard_map/ppermute | solution.py:137
  30.5 15.3 %collective-permute-start.9 = (bf16[512,256]{1,0:T(8,128)(2,1)}, bf16[512,256]{1,0:T(8,128)(2,1)S(1)}, u32[]{:S(2)}, u32[]{:S(2)}) collective-permute-start(bf16[512,256]{1,0:T(8,128)(2,1)} %get-tuple-element.56.refs_4_), channel_id=1, source_target_pairs={{0,1},{1,0},{2,3},{3,2},{4,5},{5,4},{6,7},{7,6},{8,9},{9,8},{10,11... | collective-permute-start | bytes 786440 | tf_op jit(solution)/shard_map/ppermute | solution.py:137
  30.5 9.5 %collective-permute-start.12 = (bf16[512,128]{1,0:T(8,128)(2,1)S(1)}, bf16[512,128]{1,0:T(8,128)(2,1)S(1)}, u32[]{:S(2)}, u32[]{:S(2)}) collective-permute-start(bf16[512,128]{1,0:T(8,128)(2,1)S(1)} %copy-done.31), channel_id=1, source_target_pairs={{0,1},{1,0},{2,3},{3,2},{4,5},{5,4},{6,7},{7,6},{8,9},{9,8},{10,11... | collective-permute-start | bytes 393224 | tf_op jit(solution)/shard_map/ppermute | solution.py:137
  31.0 9.1 %collective-permute-start.13 = (bf16[512,128]{1,0:T(8,128)(2,1)S(1)}, bf16[512,128]{1,0:T(8,128)(2,1)S(1)}, u32[]{:S(2)}, u32[]{:S(2)}) collective-permute-start(bf16[512,128]{1,0:T(8,128)(2,1)S(1)} %copy-done.30), channel_id=1, source_target_pairs={{0,2},{1,3},{2,0},{3,1},{4,6},{5,7},{6,4},{7,5},{8,10},{9,11},{10,... | collective-permute-start | bytes 393224 | tf_op jit(solution)/shard_map/ppermute | solution.py:137
  38.2 16.5 %collective-permute-start.11 = (bf16[512,256]{1,0:T(8,128)(2,1)S(1)}, bf16[512,256]{1,0:T(8,128)(2,1)S(1)}, u32[]{:S(2)}, u32[]{:S(2)}) collective-permute-start(bf16[512,256]{1,0:T(8,128)(2,1)S(1)} %collective-permute-done.10.refs_6_.refs_4_), channel_id=1, source_target_pairs={{0,1},{1,0},{2,3},{3,2},{4,5},{5,4},{6,7},{7,6},{8,9},{9,8},{10,11... | collective-permute-start | bytes 786440 | tf_op jit(solution)/shard_map/ppermute | solution.py:137
  40.0 13.7 %collective-permute-start.6 = (bf16[128,512]{1,0:T(8,128)(2,1)}, bf16[128,512]{1,0:T(8,128)(2,1)S(1)}, u32[]{:S(2)}, u32[]{:S(2)}) collective-permute-start(bf16[128,512]{1,0:T(8,128)(2,1)} %get-tuple-element.53), channel_id=1, source_target_pairs={{0,1},{1,0},{2,3},{3,2},{4,5},{5,4},{6,7},{7,6},{8,9},{9,8},{10,11... | collective-permute-start | bytes 393224 | tf_op jit(solution)/shard_map/ppermute | solution.py:137
  40.1 13.8 %collective-permute-start.7 = (bf16[128,512]{1,0:T(8,128)(2,1)}, bf16[128,512]{1,0:T(8,128)(2,1)S(1)}, u32[]{:S(2)}, u32[]{:S(2)}) collective-permute-start(bf16[128,512]{1,0:T(8,128)(2,1)} %get-tuple-element.54), channel_id=1, source_target_pairs={{0,2},{1,3},{2,0},{3,1},{4,6},{5,7},{6,4},{7,5},{8,10},{9,11},{10,... | collective-permute-start | bytes 393224 | tf_op jit(solution)/shard_map/ppermute | solution.py:137
  43.9 15.6 %collective-permute-start.8 = (bf16[128,512]{1,0:T(8,128)(2,1)}, bf16[128,512]{1,0:T(8,128)(2,1)S(1)}, u32[]{:S(2)}, u32[]{:S(2)}) collective-permute-start(bf16[128,512]{1,0:T(8,128)(2,1)} %get-tuple-element.55), channel_id=1, source_target_pairs={{0,3},{1,2},{2,1},{3,0},{4,7},{5,6},{6,5},{7,4},{8,11},{9,10},{10,... | collective-permute-start | bytes 393224 | tf_op jit(solution)/shard_map/ppermute | solution.py:137
  49.1 13.3 %collective-permute-start.15 = (bf16[64,512]{1,0:T(8,128)(2,1)}, bf16[64,512]{1,0:T(8,128)(2,1)S(1)}, u32[]{:S(2)}, u32[]{:S(2)}) collective-permute-start(bf16[64,512]{1,0:T(8,128)(2,1)} %get-tuple-element.64), channel_id=1, source_target_pairs={{0,28},{4,24},{8,20},{12,16},{16,12},{20,8},{24,4},{28,0},{1,29},{... | collective-permute-start | bytes 196616 | tf_op jit(solution)/shard_map/ppermute | solution.py:137
  53.7 8.9 %collective-permute-start.16 = (bf16[64,512]{1,0:T(8,128)(2,1)}, bf16[64,512]{1,0:T(8,128)(2,1)S(1)}, u32[]{:S(2)}, u32[]{:S(2)}) collective-permute-start(bf16[64,512]{1,0:T(8,128)(2,1)} %get-tuple-element.65), channel_id=1, source_target_pairs={{0,24},{4,28},{8,16},{12,20},{16,8},{20,12},{24,0},{28,4},{1,25},{... | collective-permute-start | bytes 196616 | tf_op jit(solution)/shard_map/ppermute | solution.py:137
  53.9 9.3 %collective-permute-start.17 = (bf16[64,512]{1,0:T(8,128)(2,1)}, bf16[64,512]{1,0:T(8,128)(2,1)S(1)}, u32[]{:S(2)}, u32[]{:S(2)}) collective-permute-start(bf16[64,512]{1,0:T(8,128)(2,1)} %get-tuple-element.66), channel_id=1, source_target_pairs={{0,20},{4,16},{8,28},{12,24},{16,4},{20,0},{24,12},{28,8},{1,21},{... | collective-permute-start | bytes 196616 | tf_op jit(solution)/shard_map/ppermute | solution.py:137
  54.7 13.1 %collective-permute-start.18 = (bf16[64,512]{1,0:T(8,128)(2,1)}, bf16[64,512]{1,0:T(8,128)(2,1)S(1)}, u32[]{:S(2)}, u32[]{:S(2)}) collective-permute-start(bf16[64,512]{1,0:T(8,128)(2,1)} %get-tuple-element.67), channel_id=1, source_target_pairs={{0,16},{4,20},{8,24},{12,28},{16,0},{20,4},{24,8},{28,12},{1,17},{... | collective-permute-start | bytes 196616 | tf_op jit(solution)/shard_map/ppermute | solution.py:137
  59.5 9.2 %collective-permute-start.19 = (bf16[64,512]{1,0:T(8,128)(2,1)S(1)}, bf16[64,512]{1,0:T(8,128)(2,1)S(1)}, u32[]{:S(2)}, u32[]{:S(2)}) collective-permute-start(bf16[64,512]{1,0:T(8,128)(2,1)S(1)} %copy-done.34), channel_id=1, source_target_pairs={{0,12},{4,8},{8,4},{12,0},{16,28},{20,24},{24,20},{28,16},{1,13},{... | collective-permute-start | bytes 196616 | tf_op jit(solution)/shard_map/ppermute | solution.py:137
  62.6 8.3 %collective-permute-start.21 = (bf16[64,512]{1,0:T(8,128)(2,1)S(1)}, bf16[64,512]{1,0:T(8,128)(2,1)S(1)}, u32[]{:S(2)}, u32[]{:S(2)}) collective-permute-start(bf16[64,512]{1,0:T(8,128)(2,1)S(1)} %copy-done.32), channel_id=1, source_target_pairs={{0,4},{4,0},{8,12},{12,8},{16,20},{20,16},{24,28},{28,24},{1,5},{5... | collective-permute-start | bytes 196616 | tf_op jit(solution)/shard_map/ppermute | solution.py:137
  63.2 9.9 %collective-permute-start.22 = (bf16[64,512]{1,0:T(8,128)(2,1)}, bf16[64,512]{1,0:T(8,128)(2,1)S(1)}, u32[]{:S(2)}, u32[]{:S(2)}) collective-permute-start(bf16[64,512]{1,0:T(8,128)(2,1)} %get-tuple-element.72), channel_id=1, source_target_pairs={{0,28},{4,24},{8,20},{12,16},{16,12},{20,8},{24,4},{28,0},{1,29},{... | collective-permute-start | bytes 196616 | tf_op jit(solution)/shard_map/ppermute | solution.py:137
  67.8 6.8 %collective-permute-start.23 = (bf16[64,512]{1,0:T(8,128)(2,1)}, bf16[64,512]{1,0:T(8,128)(2,1)S(1)}, u32[]{:S(2)}, u32[]{:S(2)}) collective-permute-start(bf16[64,512]{1,0:T(8,128)(2,1)} %get-tuple-element.73), channel_id=1, source_target_pairs={{0,24},{4,28},{8,16},{12,20},{16,8},{20,12},{24,0},{28,4},{1,25},{... | collective-permute-start | bytes 196616 | tf_op jit(solution)/shard_map/ppermute | solution.py:137
  68.7 10.9 %collective-permute-start.24 = (bf16[64,512]{1,0:T(8,128)(2,1)}, bf16[64,512]{1,0:T(8,128)(2,1)S(1)}, u32[]{:S(2)}, u32[]{:S(2)}) collective-permute-start(bf16[64,512]{1,0:T(8,128)(2,1)} %get-tuple-element.74), channel_id=1, source_target_pairs={{0,20},{4,16},{8,28},{12,24},{16,4},{20,0},{24,12},{28,8},{1,21},{... | collective-permute-start | bytes 196616 | tf_op jit(solution)/shard_map/ppermute | solution.py:137
  68.7 10.9 %collective-permute-start.25 = (bf16[64,512]{1,0:T(8,128)(2,1)}, bf16[64,512]{1,0:T(8,128)(2,1)S(1)}, u32[]{:S(2)}, u32[]{:S(2)}) collective-permute-start(bf16[64,512]{1,0:T(8,128)(2,1)} %get-tuple-element.75), channel_id=1, source_target_pairs={{0,16},{4,20},{8,24},{12,28},{16,0},{20,4},{24,8},{28,12},{1,17},{... | collective-permute-start | bytes 196616 | tf_op jit(solution)/shard_map/ppermute | solution.py:137
  70.9 8.7 %collective-permute-start.26 = (bf16[64,512]{1,0:T(8,128)(2,1)}, bf16[64,512]{1,0:T(8,128)(2,1)S(1)}, u32[]{:S(2)}, u32[]{:S(2)}) collective-permute-start(bf16[64,512]{1,0:T(8,128)(2,1)} %get-tuple-element.76), channel_id=1, source_target_pairs={{0,12},{4,8},{8,4},{12,0},{16,28},{20,24},{24,20},{28,16},{1,13},{... | collective-permute-start | bytes 196616 | tf_op jit(solution)/shard_map/ppermute | solution.py:137
  (42 other events, 222.1 us)
where the time goes:
time: 82.6 us; the launch traced here: 82.2 us
  starting transfers between devices  37.9 us (46%)
  Pallas kernels  21.5 us (26%)
  waiting for transfers between devices  19.5 us (24%)
  local copies, waits for them, and re-layouts  2.4 us (3%)
  between operations  0.91 us (1%)
    ppermute x29, starting transfers between devices, swapped(): lax.ppermute(value, axis, [(source, source ^ distance) for source in rang...  37.9 us
    pallas_call x8, Pallas kernels, call(): pl.pallas_call(body, out_shape=out_shapes, in_specs=specs, out_specs=[vme...  21.5 us
    ppermute x29, waiting for transfers between devices, swapped(): lax.ppermute(value, axis, [(source, source ^ distance) for source in rang...  19.5 us
    unnamed x74, local copies, waits for them, and re-layouts  2.4 us
  transfers between devices with their start and end apart: 29, of which 3 were waited for; matrix products, arithmetic and copies ran while one was open for 0% of the time, Pallas kernels for 14%

commit v1 on v0

--- a/solution.py
+++ b/solution.py
@@ -325,56 +325,56 @@
     return (outs[0], outs[1:])
 
 
-def summed(own, parts):
-    def sum_parts(own_ref, *refs):
-        total = own_ref[...]
-        for part_ref in refs[:-1]:
-            total = total + part_ref[...].astype(jnp.float32)
-        refs[-1][...] = total
-
-    return call(sum_parts, [shaped(own.shape, jnp.float32)], (own, *parts), 0)[0]
-
-
-def summed_last(place, done, own, parts, count):
-    rows, width = own.shape
-
-    def sum_last_parts(place_ref, *refs):
-        done_refs, own_ref = (refs[: len(done)], refs[len(done)])
-        part_refs, key_ref, value_ref = (refs[len(done) + 1 : -2], refs[-2], refs[-1])
-        last = own_ref[...]
-        for part_ref in part_refs:
-            last = last + part_ref[...].astype(jnp.float32)
-        pieces = [ref[...] for ref in done_refs] + [last]
-        for index, piece in enumerate(pieces):
-            for column in range(width // (2 * DH)):
-                shift = index * (width // (2 * DH)) + column
-                head = pl.multiple_of((place_ref[0] ^ shift) * DH, DH)
-                first = column * 2 * DH
-                key_ref[:, pl.ds(head, DH)] = piece[:, first : first + DH]
-                value_ref[:, pl.ds(head, DH)] = piece[:, first + DH : first + 2 * DH]
-
-    shape = shaped((rows, count * DH), jnp.float32)
-    return call(sum_last_parts, [shape] * 2, (place, *done, own, *parts), 1)
-
-
-def joined_rows(place, query_parts, tokens):
+def finished(place, groups, query_parts, tokens):
     count = len(query_parts)
-    rows, width = query_parts[0].shape
-
-    def join_rows(place_ref, *refs):
-        part_refs, token_refs = (refs[:count], refs[count : 2 * count])
-        query_ref, key_ref, value_ref = refs[2 * count :]
+    rows, query_width = query_parts[0].shape
+    own_rows, width = groups[0][0].shape
+    sizes = [1 + len(parts) for _, parts in groups]
+    heads = width // (2 * DH)
+
+    def finish(place_ref, *refs):
+        query_ref, key_ref, value_ref, key_sum_ref, value_sum_ref = refs[-5:]
+        first_ref = 0
+        for index, size in enumerate(sizes):
+            group_refs = refs[first_ref : first_ref + size]
+            first_ref += size
+            for column in range(heads):
+                head = pl.multiple_of((place_ref[0] ^ (index * heads + column)) * DH, DH)
+                for offset, out_ref in enumerate((key_sum_ref, value_sum_ref)):
+                    part = pl.ds((2 * column + offset) * DH, DH)
+                    total = group_refs[0][:, part]
+                    for part_ref in group_refs[1:]:
+                        total = total + part_ref[:, part].astype(jnp.float32)
+                    out_ref[:, pl.ds(head, DH)] = total
+        part_refs = refs[first_ref : first_ref + count]
+        token_refs = refs[first_ref + count : first_ref + 2 * count]
         for distance in range(count):
             peer = place_ref[0] ^ distance
-            wide = pl.ds(pl.multiple_of(peer * width, width), width)
+            wide = pl.ds(pl.multiple_of(peer * query_width, query_width), query_width)
             thin = pl.ds(pl.multiple_of(peer * DH, DH), DH)
-            mine = slice(distance * rows, (distance + 1) * rows)
             query_ref[:, wide] = part_refs[distance][...]
-            key_ref[:, thin] = token_refs[distance][mine, :DH]
-            value_ref[:, thin] = token_refs[distance][mine, DH:]
-
-    shapes = [shaped((rows, count * width))] + [shaped((rows, count * DH))] * 2
-    return call(join_rows, shapes, (place, *query_parts, *tokens), 1)
+            key_ref[:, thin] = token_refs[distance][:, :DH]
+            value_ref[:, thin] = token_refs[distance][:, DH:]
+
+    operands = [place]
+    for own, parts in groups:
+        operands += [own, *parts]
+    operands += [*query_parts, *tokens]
+    specs = [smem()]
+    specs += [pl.BlockSpec(held.shape, lambda step: (0, 0)) for held in operands[1:-count]]
+    specs += [
+        pl.BlockSpec((rows, 2 * DH), lambda step, index=index: (index, 0)) for index in range(count)
+    ]
+    shapes = [shaped((rows, count * query_width))] + [shaped((rows, count * DH))] * 2
+    shapes += [shaped((own_rows, count * DH), jnp.float32)] * 2
+    return pl.pallas_call(
+        finish,
+        grid=(1,),
+        out_shape=shapes,
+        in_specs=specs,
+        out_specs=[pl.BlockSpec(shape.shape, lambda step: (0, 0)) for shape in shapes],
+        name="finish",
+    )(*operands)
 
 
 def head_shards(hidden_in, queries, key_states, value_states, grad_out, log_sums, deltas, block_order):
@@ -406,7 +406,7 @@
         for distance in sorted(held):
             held[distance ^ step] = swapped(held[distance], "seq", step)
         step //= 2
-    done = []
+    groups = []
     for group in range(2):
         some = [(shift, held[shift]) for shift in range(group * half, (group + 1) * half)]
         own, parts = weight_parts(owner, features, some, owners)
@@ -414,13 +414,13 @@
             swapped(part, "batch", index + 1)
             for index, part in reversed(list(enumerate(parts)))
         ]
-        if group == 0:
-            done.append(summed(own, parts))
+        groups.append((own, parts))
     for distance in far_first:
         query_parts[distance] = swapped(query_parts[distance], "seq", distance)
     all_tokens = [held[distance] for distance in range(count)]
-    grad_queries, grad_keys, grad_values = joined_rows(place, query_parts, all_tokens)
-    key_wgrad, value_wgrad = summed_last(place, done, own, parts, count)
+    grad_queries, grad_keys, grad_values, key_wgrad, value_wgrad = finished(
+        place, groups, query_parts, all_tokens
+    )
     return (grad_queries[None], grad_keys[None], grad_values[None], key_wgrad, value_wgrad)
 
 

time: 82.6 us -> 82.5 us (level)
  waiting for transfers between devices: 19.5 us -> 23.1 us
  Pallas kernels: 21.5 us -> 18 us
    pallas_call x8 -> x5, Pallas kernels: 21.5 us -> 15.4 us  [call(): pl.pallas_call(body, out_shape=out_shapes, in_specs=specs, out_specs=[vme...]
    ppermute x29, waiting for transfers between devices: 19.5 us -> 23.1 us  [swapped(): lax.ppermute(value, axis, [(source, source ^ distance) for source in rang...]
    pallas_call x0 -> x1, Pallas kernels: none -> 2.6 us  [finished(): pl.pallas_call(finish, grid=(1,), out_shape=shapes, in_specs=specs, out_s...]
  transfers between devices with their start and end apart: 29 -> 29, of which waited for: 3 -> 6; matrix products, arithmetic and copies ran while one was open for 0% -> 0% of each run, Pallas kernels for 14% -> 9%
where the time goes in v1:
time: 82.5 us; the launch traced here: 82.2 us
  starting transfers between devices  37.9 us (46%)
  waiting for transfers between devices  23.1 us (28%)
  Pallas kernels  18 us (22%)
  local copies, waits for them, and re-layouts  2.25 us (3%)
  between operations  0.91 us (1%)
    ppermute x29, starting transfers between devices, swapped(): lax.ppermute(value, axis, [(source, source ^ distance) for source in rang...  37.9 us
    ppermute x29, waiting for transfers between devices, swapped(): lax.ppermute(value, axis, [(source, source ^ distance) for source in rang...  23.1 us
    pallas_call x5, Pallas kernels, call(): pl.pallas_call(body, out_shape=out_shapes, in_specs=specs, out_specs=[vme...  15.4 us
    pallas_call x1, Pallas kernels, finished(): pl.pallas_call(finish, grid=(1,), out_shape=shapes, in_specs=specs, out_s...  2.6 us
    unnamed x74, local copies, waits for them, and re-layouts  2.25 us
  transfers between devices with their start and end apart: 29, of which 6 were waited for; matrix products, arithmetic and copies ran while one was open for 0% of the time, Pallas kernels for 9%

profile of v1, /device:TPU:0, one launch (start us, length us, event | category | flops | bytes accessed | tf_op | source)
XLA Modules:
  0.0 82.2 jit_solution(11017125835986893864)
XLA Ops:
  0.6 2.5 %shard_map.119 = (bf16[128,1280]{1,0:T(8,128)(2,1)}, bf16[128,1280]{1,0:T(8,128)(2,1)}, bf16[128,1280]{1,0:T(8,128)(2,1)}, bf16[128,1280]{1,0:T(8,128)(2,1)}, f3...) custom-call(s32[1]{0:T(128)} %bitcast.place_ref, bf16[128,2048]{1,0:T(8,128)(2,1)} %bitcast.12, ...), custom_call_target="tpu_custom_call" | custom-call | tf_op jit(solution)/shard_map/pallas_call | solution.py:156
  3.7 2.6 %collective-permute-start.4 = (bf16[128,1280]{1,0:T(8,128)(2,1)}, bf16[128,1280]{1,0:T(8,128)(2,1)S(1)}, u32[]{:S(2)}, u32[]{:S(2)}) collective-permute-start(bf16[128,1280]{1,0:T(8,128)(2,1)} %get-tuple-element.49), channel_id=1, source_target_pairs={{0,2},{1,3},{2,0},{3,1},{4,6},{5,7},{6,4},{7,5},{8,10},{9,11},{10,... | collective-permute-start | bytes 983048 | tf_op jit(solution)/shard_map/ppermute | solution.py:137
  6.4 1.9 %collective-permute-start.7 = (f32[8,128]{1,0:T(8,128)S(1)}, f32[8,128]{1,0:T(8,128)S(1)}, u32[]{:S(2)}, u32[]{:S(2)}) collective-permute-start(f32[8,128]{1,0:T(8,128)S(1)} %copy-done.36), channel_id=1, source_target_pairs={{0,2},{1,3},{2,0},{3,1},{4,6},{5,7},{6,4},{7,5},{8,10},{9,11},{10,... | collective-permute-start | bytes 12296 | tf_op jit(solution)/shard_map/ppermute | solution.py:137
  9.4 2.0 %shard_map.120 = (bf16[512,128]{1,0:T(8,128)(2,1)}, bf16[512,128]{1,0:T(8,128)(2,1)}, bf16[512,128]{1,0:T(8,128)(2,1)}, bf16[512,128]{1,0:T(8,128)(2,1)}) custom-call(s32[1]{0:T(128)} %bitcast.place_ref, bf16[128,2048]{1,0:T(8,128)(2,1)} %bitcast.14, bf16[128,1280]{1,0:T(8,128)(2,1)} %get-tuple-element.43._.refs_0_), custom_call_target="tpu_custom_call" | custom-call | tf_op jit(solution)/shard_map/pallas_call | solution.py:156
  11.4 10.5 %collective-permute-done.7.refs_6_ = f32[8,128]{1,0:T(8,128)S(1)} collective-permute-done((f32[8,128]{1,0:T(8,128)S(1)}, f32[8,128]{1,0:T(8,128)S(1)}, u32[]{:S(2)}, u32[]{:S(2)}) %collective-permute-start.7) | collective-permute-done | bytes 4128 | tf_op jit(solution)/shard_map/ppermute | solution.py:137
  22.9 5.9 %shard_map.121 = (bf16[128,512]{1,0:T(8,128)(2,1)}, bf16[128,512]{1,0:T(8,128)(2,1)}, bf16[128,512]{1,0:T(8,128)(2,1)}, bf16[128,512]{1,0:T(8,128)(2,1)}, bf16[512,256]{1,0:T(8,128)(2,1)}) custom-call(s32[1]{0:T(128)} %bitcast.place_ref, s32[8]{0:T(128)} %order_ref.1, bf16[128,1280]{1,0:T(8,128)(2,1)} %get-tuple-element.43._.refs_0_, ...), custom_call_target="tpu_custom_call" | custom-call | tf_op jit(solution)/shard_map/pallas_call | solution.py:156
  28.8 1.7 %collective-permute-start.17 = (bf16[512,256]{1,0:T(8,128)(2,1)}, bf16[512,256]{1,0:T(8,128)(2,1)S(1)}, u32[]{:S(2)}, u32[]{:S(2)}) collective-permute-start(bf16[512,256]{1,0:T(8,128)(2,1)} %get-tuple-element.55.refs_4_.refs_20_), channel_id=1, source_target_pairs={{0,2},{1,3},{2,0},{3,1},{4,6},{5,7},{6,4},{7,5},{8,10},{9,11},{10,... | collective-permute-start | bytes 786440 | tf_op jit(solution)/shard_map/ppermute | solution.py:137
  31.3 6.8 %collective-permute-done.17.refs_4_.refs_22_ = bf16[512,256]{1,0:T(8,128)(2,1)S(1)} collective-permute-done((bf16[512,256]{1,0:T(8,128)(2,1)}, bf16[512,256]{1,0:T(8,128)(2,1)S(1)}, u32[]{:S(2)}, u32[]{:S(2)}) %collective-permute-start.17) | collective-permute-done | bytes 262176 | tf_op jit(solution)/shard_map/ppermute | solution.py:137
  38.2 1.9 %collective-permute-start.2 = (bf16[512,128]{1,0:T(8,128)(2,1)S(1)}, bf16[512,128]{1,0:T(8,128)(2,1)S(1)}, u32[]{:S(2)}, u32[]{:S(2)}) collective-permute-start(bf16[512,128]{1,0:T(8,128)(2,1)S(1)} %copy-done.29), channel_id=1, source_target_pairs={{0,3},{1,2},{2,1},{3,0},{4,7},{5,6},{6,5},{7,4},{8,11},{9,10},{10,... | collective-permute-start | bytes 393224 | tf_op jit(solution)/shard_map/ppermute | solution.py:137
  40.1 1.7 %collective-permute-start.27 = (bf16[128,512]{1,0:T(8,128)(2,1)}, bf16[128,512]{1,0:T(8,128)(2,1)S(1)}, u32[]{:S(2)}, u32[]{:S(2)}) collective-permute-start(bf16[128,512]{1,0:T(8,128)(2,1)} %get-tuple-element.74), channel_id=1, source_target_pairs={{0,2},{1,3},{2,0},{3,1},{4,6},{5,7},{6,4},{7,5},{8,10},{9,11},{10,... | collective-permute-start | bytes 393224 | tf_op jit(solution)/shard_map/ppermute | solution.py:137
  41.9 2.1 %collective-permute-done.2.refs_3_ = bf16[512,128]{1,0:T(8,128)(2,1)S(1)} collective-permute-done((bf16[512,128]{1,0:T(8,128)(2,1)S(1)}, bf16[512,128]{1,0:T(8,128)(2,1)S(1)}, u32[]{:S(2)}, u32[]{:S(2)}) %collective-permute-start.2) | collective-permute-done | bytes 131104 | tf_op jit(solution)/shard_map/ppermute | solution.py:137
  43.9 1.9 %collective-permute-start.28 = (bf16[128,512]{1,0:T(8,128)(2,1)}, bf16[128,512]{1,0:T(8,128)(2,1)S(1)}, u32[]{:S(2)}, u32[]{:S(2)}) collective-permute-start(bf16[128,512]{1,0:T(8,128)(2,1)} %get-tuple-element.75), channel_id=1, source_target_pairs={{0,3},{1,2},{2,1},{3,0},{4,7},{5,6},{6,5},{7,4},{8,11},{9,10},{10,... | collective-permute-start | bytes 393224 | tf_op jit(solution)/shard_map/ppermute | solution.py:137
  46.5 2.5 %shard_map.122 = (f32[64,512]{1,0:T(8,128)}, bf16[64,512]{1,0:T(8,128)(2,1)}, bf16[64,512]{1,0:T(8,128)(2,1)}, bf16[64,512]{1,0:T(8,128)(2,1)}, bf16[64,512]{1,0...) custom-call(s32[1]{0:T(128)} %bitcast.1.owner_ref, ...), custom_call_target="tpu_custom_call" | custom-call | tf_op jit(solution)/shard_map/pallas_call | solution.py:156
  49.1 4.6 %collective-permute-start.10 = (bf16[64,512]{1,0:T(8,128)(2,1)}, bf16[64,512]{1,0:T(8,128)(2,1)S(1)}, u32[]{:S(2)}, u32[]{:S(2)}) collective-permute-start(bf16[64,512]{1,0:T(8,128)(2,1)} %get-tuple-element.57), channel_id=1, source_target_pairs={{0,28},{4,24},{8,20},{12,16},{16,12},{20,8},{24,4},{28,0},{1,29},{... | collective-permute-start | bytes 196616 | tf_op jit(solution)/shard_map/ppermute | solution.py:137
  54.7 2.2 %collective-permute-start.13 = (bf16[64,512]{1,0:T(8,128)(2,1)}, bf16[64,512]{1,0:T(8,128)(2,1)S(1)}, u32[]{:S(2)}, u32[]{:S(2)}) collective-permute-start(bf16[64,512]{1,0:T(8,128)(2,1)} %get-tuple-element.60), channel_id=1, source_target_pairs={{0,16},{4,20},{8,24},{12,28},{16,0},{20,4},{24,8},{28,12},{1,17},{... | collective-permute-start | bytes 196616 | tf_op jit(solution)/shard_map/ppermute | solution.py:137
  56.9 2.6 %shard_map.123 = (f32[64,512]{1,0:T(8,128)}, bf16[64,512]{1,0:T(8,128)(2,1)}, bf16[64,512]{1,0:T(8,128)(2,1)}, bf16[64,512]{1,0:T(8,128)(2,1)}, bf16[64,512]{1,0...) custom-call(s32[1]{0:T(128)} %bitcast.1.owner_ref, ...), custom_call_target="tpu_custom_call" | custom-call | tf_op jit(solution)/shard_map/pallas_call | solution.py:156
  59.5 2.8 %collective-permute-start.14 = (bf16[64,512]{1,0:T(8,128)(2,1)S(1)}, bf16[64,512]{1,0:T(8,128)(2,1)S(1)}, u32[]{:S(2)}, u32[]{:S(2)}) collective-permute-start(bf16[64,512]{1,0:T(8,128)(2,1)S(1)} %copy-done.34), channel_id=1, source_target_pairs={{0,12},{4,8},{8,4},{12,0},{16,28},{20,24},{24,20},{28,16},{1,13},{... | collective-permute-start | bytes 196616 | tf_op jit(solution)/shard_map/ppermute | solution.py:137
  63.2 4.5 %collective-permute-start.19 = (bf16[64,512]{1,0:T(8,128)(2,1)}, bf16[64,512]{1,0:T(8,128)(2,1)S(1)}, u32[]{:S(2)}, u32[]{:S(2)}) collective-permute-start(bf16[64,512]{1,0:T(8,128)(2,1)} %get-tuple-element.65), channel_id=1, source_target_pairs={{0,28},{4,24},{8,20},{12,16},{16,12},{20,8},{24,4},{28,0},{1,29},{... | collective-permute-start | bytes 196616 | tf_op jit(solution)/shard_map/ppermute | solution.py:137
  68.7 2.1 %collective-permute-start.22 = (bf16[64,512]{1,0:T(8,128)(2,1)}, bf16[64,512]{1,0:T(8,128)(2,1)S(1)}, u32[]{:S(2)}, u32[]{:S(2)}) collective-permute-start(bf16[64,512]{1,0:T(8,128)(2,1)} %get-tuple-element.68), channel_id=1, source_target_pairs={{0,16},{4,20},{8,24},{12,28},{16,0},{20,4},{24,8},{28,12},{1,17},{... | collective-permute-start | bytes 196616 | tf_op jit(solution)/shard_map/ppermute | solution.py:137
  70.8 2.3 %collective-permute-start.23 = (bf16[64,512]{1,0:T(8,128)(2,1)}, bf16[64,512]{1,0:T(8,128)(2,1)S(1)}, u32[]{:S(2)}, u32[]{:S(2)}) collective-permute-start(bf16[64,512]{1,0:T(8,128)(2,1)} %get-tuple-element.69), channel_id=1, source_target_pairs={{0,12},{4,8},{8,4},{12,0},{16,28},{20,24},{24,20},{28,16},{1,13},{... | collective-permute-start | bytes 196616 | tf_op jit(solution)/shard_map/ppermute | solution.py:137
  73.1 1.4 %collective-permute-start.24 = (bf16[64,512]{1,0:T(8,128)(2,1)}, bf16[64,512]{1,0:T(8,128)(2,1)S(1)}, u32[]{:S(2)}, u32[]{:S(2)}) collective-permute-start(bf16[64,512]{1,0:T(8,128)(2,1)} %get-tuple-element.70), channel_id=1, source_target_pairs={{0,8},{4,12},{8,0},{12,4},{16,24},{20,28},{24,16},{28,20},{1,9},{5... | collective-permute-start | bytes 196616 | tf_op jit(solution)/shard_map/ppermute | solution.py:137
  75.3 1.5 %collective-permute-done.21.refs_11_ = bf16[64,512]{1,0:T(8,128)(2,1)S(1)} collective-permute-done((bf16[64,512]{1,0:T(8,128)(2,1)}, bf16[64,512]{1,0:T(8,128)(2,1)S(1)}, u32[]{:S(2)}, u32[]{:S(2)}) %collective-permute-start.21) | collective-permute-done | bytes 65568 | tf_op jit(solution)/shard_map/ppermute | solution.py:137
  76.8 1.6 %collective-permute-done.22.refs_12_ = bf16[64,512]{1,0:T(8,128)(2,1)S(1)} collective-permute-done((bf16[64,512]{1,0:T(8,128)(2,1)}, bf16[64,512]{1,0:T(8,128)(2,1)S(1)}, u32[]{:S(2)}, u32[]{:S(2)}) %collective-permute-start.22) | collective-permute-done | bytes 65568 | tf_op jit(solution)/shard_map/ppermute | solution.py:137
  79.6 2.6 %finish.1 = (bf16[128,2048]{1,0:T(8,128)(2,1)}, bf16[128,512]{1,0:T(8,128)(2,1)}, bf16[128,512]{1,0:T(8,128)(2,1)}, f32[64,512]{1,0:T(8,128)}, f32[64,512]{1,0:T(8,128)}) custom-call(s32[1]{0:T(128)} %bitcast.place_ref, f32[64,512]{1,0:T(8,128)} %get-tuple-element.56.refs_0_, bf16[64,512]{1,0:T(8,128)(2,1)} %copy-done.12, bf16[64,512]{1,0:T(8,128)(2,1)} %copy-done.13, ...), custom_call_target="tpu_custom_call" | custom-call | tf_op jit(solution)/shard_map/finish/pallas_call | solution.py:370
  (114 shorter events, 9.1 us)
Async XLA Ops:
  3.1 18.8 %collective-permute-start.3 = (bf16[128,1280]{1,0:T(8,128)(2,1)}, bf16[128,1280]{1,0:T(8,128)(2,1)S(1)}, u32[]{:S(2)}, u32[]{:S(2)}) collective-permute-start(bf16[128,1280]{1,0:T(8,128)(2,1)} %get-tuple-element.48), channel_id=1, source_target_pairs={{0,1},{1,0},{2,3},{3,2},{4,5},{5,4},{6,7},{7,6},{8,9},{9,8},{10,11... | collective-permute-start | bytes 983048 | tf_op jit(solution)/shard_map/ppermute | solution.py:137
  3.7 18.3 %collective-permute-start.4 = (bf16[128,1280]{1,0:T(8,128)(2,1)}, bf16[128,1280]{1,0:T(8,128)(2,1)S(1)}, u32[]{:S(2)}, u32[]{:S(2)}) collective-permute-start(bf16[128,1280]{1,0:T(8,128)(2,1)} %get-tuple-element.49), channel_id=1, source_target_pairs={{0,2},{1,3},{2,0},{3,1},{4,6},{5,7},{6,4},{7,5},{8,10},{9,11},{10,... | collective-permute-start | bytes 983048 | tf_op jit(solution)/shard_map/ppermute | solution.py:137
  6.2 15.7 %collective-permute-start.5 = (bf16[128,1280]{1,0:T(8,128)(2,1)}, bf16[128,1280]{1,0:T(8,128)(2,1)S(1)}, u32[]{:S(2)}, u32[]{:S(2)}) collective-permute-start(bf16[128,1280]{1,0:T(8,128)(2,1)} %get-tuple-element.50), channel_id=1, source_target_pairs={{0,3},{1,2},{2,1},{3,0},{4,7},{5,6},{6,5},{7,4},{8,11},{9,10},{10,... | collective-permute-start | bytes 983048 | tf_op jit(solution)/shard_map/ppermute | solution.py:137
  6.4 15.5 %collective-permute-start.7 = (f32[8,128]{1,0:T(8,128)S(1)}, f32[8,128]{1,0:T(8,128)S(1)}, u32[]{:S(2)}, u32[]{:S(2)}) collective-permute-start(f32[8,128]{1,0:T(8,128)S(1)} %copy-done.36), channel_id=1, source_target_pairs={{0,2},{1,3},{2,0},{3,1},{4,6},{5,7},{6,4},{7,5},{8,10},{9,11},{10,... | collective-permute-start | bytes 12296 | tf_op jit(solution)/shard_map/ppermute | solution.py:137
  8.4 13.5 %collective-permute-start.8 = (f32[8,128]{1,0:T(8,128)S(1)}, f32[8,128]{1,0:T(8,128)S(1)}, u32[]{:S(2)}, u32[]{:S(2)}) collective-permute-start(f32[8,128]{1,0:T(8,128)S(1)} %copy-done.35), channel_id=1, source_target_pairs={{0,3},{1,2},{2,1},{3,0},{4,7},{5,6},{6,5},{7,4},{8,11},{9,10},{10,... | collective-permute-start | bytes 12296 | tf_op jit(solution)/shard_map/ppermute | solution.py:137
  28.8 9.4 %collective-permute-start.17 = (bf16[512,256]{1,0:T(8,128)(2,1)}, bf16[512,256]{1,0:T(8,128)(2,1)S(1)}, u32[]{:S(2)}, u32[]{:S(2)}) collective-permute-start(bf16[512,256]{1,0:T(8,128)(2,1)} %get-tuple-element.55.refs_4_.refs_20_), channel_id=1, source_target_pairs={{0,2},{1,3},{2,0},{3,1},{4,6},{5,7},{6,4},{7,5},{8,10},{9,11},{10,... | collective-permute-start | bytes 786440 | tf_op jit(solution)/shard_map/ppermute | solution.py:137
  30.5 15.3 %collective-permute-start.9 = (bf16[512,256]{1,0:T(8,128)(2,1)}, bf16[512,256]{1,0:T(8,128)(2,1)S(1)}, u32[]{:S(2)}, u32[]{:S(2)}) collective-permute-start(bf16[512,256]{1,0:T(8,128)(2,1)} %get-tuple-element.55.refs_4_.refs_20_), channel_id=1, source_target_pairs={{0,1},{1,0},{2,3},{3,2},{4,5},{5,4},{6,7},{7,6},{8,9},{9,8},{10,11... | collective-permute-start | bytes 786440 | tf_op jit(solution)/shard_map/ppermute | solution.py:137
  30.5 9.5 %collective-permute-start = (bf16[512,128]{1,0:T(8,128)(2,1)S(1)}, bf16[512,128]{1,0:T(8,128)(2,1)S(1)}, u32[]{:S(2)}, u32[]{:S(2)}) collective-permute-start(bf16[512,128]{1,0:T(8,128)(2,1)S(1)} %copy-done.31), channel_id=1, source_target_pairs={{0,1},{1,0},{2,3},{3,2},{4,5},{5,4},{6,7},{7,6},{8,9},{9,8},{10,11... | collective-permute-start | bytes 393224 | tf_op jit(solution)/shard_map/ppermute | solution.py:137
  31.0 9.1 %collective-permute-start.1 = (bf16[512,128]{1,0:T(8,128)(2,1)S(1)}, bf16[512,128]{1,0:T(8,128)(2,1)S(1)}, u32[]{:S(2)}, u32[]{:S(2)}) collective-permute-start(bf16[512,128]{1,0:T(8,128)(2,1)S(1)} %copy-done.30), channel_id=1, source_target_pairs={{0,2},{1,3},{2,0},{3,1},{4,6},{5,7},{6,4},{7,5},{8,10},{9,11},{10,... | collective-permute-start | bytes 393224 | tf_op jit(solution)/shard_map/ppermute | solution.py:137
  38.2 16.5 %collective-permute-start.18 = (bf16[512,256]{1,0:T(8,128)(2,1)S(1)}, bf16[512,256]{1,0:T(8,128)(2,1)S(1)}, u32[]{:S(2)}, u32[]{:S(2)}) collective-permute-start(bf16[512,256]{1,0:T(8,128)(2,1)S(1)} %collective-permute-done.17.refs_4_.refs_22_), channel_id=1, source_target_pairs={{0,1},{1,0},{2,3},{3,2},{4,5},{5,4},{6,7},{7,6},{8,9},{9,8},{10,11... | collective-permute-start | bytes 786440 | tf_op jit(solution)/shard_map/ppermute | solution.py:137
  40.0 13.6 %collective-permute-start.26 = (bf16[128,512]{1,0:T(8,128)(2,1)}, bf16[128,512]{1,0:T(8,128)(2,1)S(1)}, u32[]{:S(2)}, u32[]{:S(2)}) collective-permute-start(bf16[128,512]{1,0:T(8,128)(2,1)} %get-tuple-element.73), channel_id=1, source_target_pairs={{0,1},{1,0},{2,3},{3,2},{4,5},{5,4},{6,7},{7,6},{8,9},{9,8},{10,11... | collective-permute-start | bytes 393224 | tf_op jit(solution)/shard_map/ppermute | solution.py:137
  40.1 13.7 %collective-permute-start.27 = (bf16[128,512]{1,0:T(8,128)(2,1)}, bf16[128,512]{1,0:T(8,128)(2,1)S(1)}, u32[]{:S(2)}, u32[]{:S(2)}) collective-permute-start(bf16[128,512]{1,0:T(8,128)(2,1)} %get-tuple-element.74), channel_id=1, source_target_pairs={{0,2},{1,3},{2,0},{3,1},{4,6},{5,7},{6,4},{7,5},{8,10},{9,11},{10,... | collective-permute-start | bytes 393224 | tf_op jit(solution)/shard_map/ppermute | solution.py:137
  43.9 15.5 %collective-permute-start.28 = (bf16[128,512]{1,0:T(8,128)(2,1)}, bf16[128,512]{1,0:T(8,128)(2,1)S(1)}, u32[]{:S(2)}, u32[]{:S(2)}) collective-permute-start(bf16[128,512]{1,0:T(8,128)(2,1)} %get-tuple-element.75), channel_id=1, source_target_pairs={{0,3},{1,2},{2,1},{3,0},{4,7},{5,6},{6,5},{7,4},{8,11},{9,10},{10,... | collective-permute-start | bytes 393224 | tf_op jit(solution)/shard_map/ppermute | solution.py:137
  49.1 13.2 %collective-permute-start.10 = (bf16[64,512]{1,0:T(8,128)(2,1)}, bf16[64,512]{1,0:T(8,128)(2,1)S(1)}, u32[]{:S(2)}, u32[]{:S(2)}) collective-permute-start(bf16[64,512]{1,0:T(8,128)(2,1)} %get-tuple-element.57), channel_id=1, source_target_pairs={{0,28},{4,24},{8,20},{12,16},{16,12},{20,8},{24,4},{28,0},{1,29},{... | collective-permute-start | bytes 196616 | tf_op jit(solution)/shard_map/ppermute | solution.py:137
  53.6 8.9 %collective-permute-start.11 = (bf16[64,512]{1,0:T(8,128)(2,1)}, bf16[64,512]{1,0:T(8,128)(2,1)S(1)}, u32[]{:S(2)}, u32[]{:S(2)}) collective-permute-start(bf16[64,512]{1,0:T(8,128)(2,1)} %get-tuple-element.58), channel_id=1, source_target_pairs={{0,24},{4,28},{8,16},{12,20},{16,8},{20,12},{24,0},{28,4},{1,25},{... | collective-permute-start | bytes 196616 | tf_op jit(solution)/shard_map/ppermute | solution.py:137
  53.9 9.3 %collective-permute-start.12 = (bf16[64,512]{1,0:T(8,128)(2,1)}, bf16[64,512]{1,0:T(8,128)(2,1)S(1)}, u32[]{:S(2)}, u32[]{:S(2)}) collective-permute-start(bf16[64,512]{1,0:T(8,128)(2,1)} %get-tuple-element.59), channel_id=1, source_target_pairs={{0,20},{4,16},{8,28},{12,24},{16,4},{20,0},{24,12},{28,8},{1,21},{... | collective-permute-start | bytes 196616 | tf_op jit(solution)/shard_map/ppermute | solution.py:137
  54.7 13.0 %collective-permute-start.13 = (bf16[64,512]{1,0:T(8,128)(2,1)}, bf16[64,512]{1,0:T(8,128)(2,1)S(1)}, u32[]{:S(2)}, u32[]{:S(2)}) collective-permute-start(bf16[64,512]{1,0:T(8,128)(2,1)} %get-tuple-element.60), channel_id=1, source_target_pairs={{0,16},{4,20},{8,24},{12,28},{16,0},{20,4},{24,8},{28,12},{1,17},{... | collective-permute-start | bytes 196616 | tf_op jit(solution)/shard_map/ppermute | solution.py:137
  59.5 9.2 %collective-permute-start.14 = (bf16[64,512]{1,0:T(8,128)(2,1)S(1)}, bf16[64,512]{1,0:T(8,128)(2,1)S(1)}, u32[]{:S(2)}, u32[]{:S(2)}) collective-permute-start(bf16[64,512]{1,0:T(8,128)(2,1)S(1)} %copy-done.34), channel_id=1, source_target_pairs={{0,12},{4,8},{8,4},{12,0},{16,28},{20,24},{24,20},{28,16},{1,13},{... | collective-permute-start | bytes 196616 | tf_op jit(solution)/shard_map/ppermute | solution.py:137
  62.6 8.3 %collective-permute-start.16 = (bf16[64,512]{1,0:T(8,128)(2,1)S(1)}, bf16[64,512]{1,0:T(8,128)(2,1)S(1)}, u32[]{:S(2)}, u32[]{:S(2)}) collective-permute-start(bf16[64,512]{1,0:T(8,128)(2,1)S(1)} %copy-done.32), channel_id=1, source_target_pairs={{0,4},{4,0},{8,12},{12,8},{16,20},{20,16},{24,28},{28,24},{1,5},{5... | collective-permute-start | bytes 196616 | tf_op jit(solution)/shard_map/ppermute | solution.py:137
  63.2 9.9 %collective-permute-start.19 = (bf16[64,512]{1,0:T(8,128)(2,1)}, bf16[64,512]{1,0:T(8,128)(2,1)S(1)}, u32[]{:S(2)}, u32[]{:S(2)}) collective-permute-start(bf16[64,512]{1,0:T(8,128)(2,1)} %get-tuple-element.65), channel_id=1, source_target_pairs={{0,28},{4,24},{8,20},{12,16},{16,12},{20,8},{24,4},{28,0},{1,29},{... | collective-permute-start | bytes 196616 | tf_op jit(solution)/shard_map/ppermute | solution.py:137
  67.7 6.8 %collective-permute-start.20 = (bf16[64,512]{1,0:T(8,128)(2,1)}, bf16[64,512]{1,0:T(8,128)(2,1)S(1)}, u32[]{:S(2)}, u32[]{:S(2)}) collective-permute-start(bf16[64,512]{1,0:T(8,128)(2,1)} %get-tuple-element.66), channel_id=1, source_target_pairs={{0,24},{4,28},{8,16},{12,20},{16,8},{20,12},{24,0},{28,4},{1,25},{... | collective-permute-start | bytes 196616 | tf_op jit(solution)/shard_map/ppermute | solution.py:137
  68.7 8.2 %collective-permute-start.21 = (bf16[64,512]{1,0:T(8,128)(2,1)}, bf16[64,512]{1,0:T(8,128)(2,1)S(1)}, u32[]{:S(2)}, u32[]{:S(2)}) collective-permute-start(bf16[64,512]{1,0:T(8,128)(2,1)} %get-tuple-element.67), channel_id=1, source_target_pairs={{0,20},{4,16},{8,28},{12,24},{16,4},{20,0},{24,12},{28,8},{1,21},{... | collective-permute-start | bytes 196616 | tf_op jit(solution)/shard_map/ppermute | solution.py:137
  68.7 9.7 %collective-permute-start.22 = (bf16[64,512]{1,0:T(8,128)(2,1)}, bf16[64,512]{1,0:T(8,128)(2,1)S(1)}, u32[]{:S(2)}, u32[]{:S(2)}) collective-permute-start(bf16[64,512]{1,0:T(8,128)(2,1)} %get-tuple-element.68), channel_id=1, source_target_pairs={{0,16},{4,20},{8,24},{12,28},{16,0},{20,4},{24,8},{28,12},{1,17},{... | collective-permute-start | bytes 196616 | tf_op jit(solution)/shard_map/ppermute | solution.py:137
  70.8 7.6 %collective-permute-start.23 = (bf16[64,512]{1,0:T(8,128)(2,1)}, bf16[64,512]{1,0:T(8,128)(2,1)S(1)}, u32[]{:S(2)}, u32[]{:S(2)}) collective-permute-start(bf16[64,512]{1,0:T(8,128)(2,1)} %get-tuple-element.69), channel_id=1, source_target_pairs={{0,12},{4,8},{8,4},{12,0},{16,28},{20,24},{24,20},{28,16},{1,13},{... | collective-permute-start | bytes 196616 | tf_op jit(solution)/shard_map/ppermute | solution.py:137
  (42 other events, 254.1 us)
